TPU v7x, 512 devices: a whole 4x8x8 slice. The times are simulated.
512 devices in a mesh: seq: 256 (over z, x, y_lo, core), head: 2 (over y_hi).
Axes of the slice: x: 4, y: 8 (y_hi: 2, y_lo: 4; y = y_hi * 4 + y_lo), z: 8, core: 2. Of those that a mesh axis runs over, the one named last changes fastest.
Arguments:
- queries: bfloat16 [32768, 2048], P('seq', 'head'), may hold values from -5 to 5
- keys: bfloat16 [32768, 2048], P('seq', 'head'), may hold values from -5 to 5
- values: bfloat16 [32768, 2048], P('seq', 'head'), may hold values from -6 to 6
- grad_out: bfloat16 [32768, 2048], P('seq', 'head'), may hold values from -6 to 6
- doc_ids: int32 [32768], P(('seq', 'head')), may hold values from 0 to 511, never falling along the last dimension, each value on 1 to 512 neighbouring positions
- loss_mask: int32 [32768], P(('seq', 'head')), may hold values 0 or 1
Outputs:
- attended: bfloat16 [32768, 2048], P('seq', 'head')
- query_grad: bfloat16 [32768, 2048], P('seq', 'head')
- key_grad: bfloat16 [32768, 2048], P('seq', 'head')
- value_grad: bfloat16 [32768, 2048], P('seq', 'head')
Inputs may be any that keep to these rules, and one draw needn't show every extreme that they name: `doc_ids`: documents are runs of consecutive tokens numbered 0, 1, 2, ... in order; each has 1 to 512 tokens.
All inputs are finite; a program needn't handle non-finite values. No bound on the sum of `loss_mask` on one device may be relied on, other than what follows from the above.
Results may differ from a plain program's by a relative error of at most 0.033.
Values may be sent and summed in bfloat16 or wider, within the bound.
A program may use at most 64 MiB of HBM per device.

v0:
```python
from functools import reduce
import math

import jax
import jax.numpy as jnp
from jax import lax
from jax.sharding import Mesh
from jax.sharding import PartitionSpec as P

HEAD_DIM = 128
REACH = 4
WINDOW = 512
SEQ = ("seq_0", "seq_1", "seq_2", "seq_3")
SEQ_HEAD = ("seq_0", "seq_1", "seq_2", "seq_3", "head")


masked_value = -1e30
big_index = 2**30


def turned_gather(arrays, axis, dims):
    turned = [jnp.moveaxis(a, dim, 0) for a, dim in zip(arrays, dims)]
    widths = [t[0].size for t in turned]
    both = jnp.concatenate([t.reshape(-1, w) for t, w in zip(turned, widths)], axis=1)
    out = lax.all_gather(both, axis, axis=0, tiled=True)
    pieces = jnp.split(out, [sum(widths[:k]) for k in range(1, len(widths))], axis=1)
    return tuple(
        (
            jnp.moveaxis(b.reshape(-1, *t.shape[1:]), 0, dim)
            for b, t, dim in zip(pieces, turned, dims)
        )
    )


def by_axis(value, axes):
    for axis in axes:
        value = lax.psum(value, axis)
    return value


def one_axis_at_a_time(value, axes):
    for axis in axes:
        value = lax.pmin(value, axis)
    return value


def shifted(block, axis, distance):
    devices = range(lax.axis_size(axis))
    route = [(i - distance, i) for i in devices if i - distance in devices]
    return lax.ppermute(block, axis, route)


def for_sending(value):

    def short(part):
        return part.astype(jnp.bfloat16) if part.dtype == jnp.float32 else part

    return jax.tree.map(short, value)


def allowed_for(q_pos, q_start, k_pos):
    later = k_pos[None, :] <= q_pos[:, None]
    inside = k_pos[None, :] > q_pos[:, None] - WINDOW
    same_doc = k_pos[None, :] >= q_start[:, None]
    return later & inside & same_doc


def by_head(rows):
    return rows.reshape(rows.shape[0], -1, HEAD_DIM)


def tile_scores(q_rows, k_rows, allowed):
    score = jnp.einsum(
        "qhd,khd->hqk", by_head(q_rows), by_head(k_rows), preferred_element_type=jnp.float32
    )
    return jnp.where(allowed[None], score * (1.0 / math.sqrt(HEAD_DIM)), masked_value)


def tile_mix(prob, v_rows):
    return jnp.einsum(
        "hqk,khd->qhd",
        prob.astype(jnp.bfloat16),
        by_head(v_rows),
        preferred_element_type=jnp.float32,
    )


def grad_of_scores(g_rows, v_rows, prob, row_delta):
    prob_grad = jnp.einsum(
        "qhd,khd->hqk", by_head(g_rows), by_head(v_rows), preferred_element_type=jnp.float32
    )
    return (prob * (prob_grad - row_delta[..., None]) * (1.0 / math.sqrt(HEAD_DIM))).astype(
        jnp.bfloat16
    )


def key_terms_of(q_rows, g_rows, k_rows, prob, score_grad):
    key_part = jnp.einsum(
        "hqk,qhd->khd", score_grad, by_head(q_rows), preferred_element_type=jnp.float32
    )
    value_part = jnp.einsum(
        "hqk,qhd->khd",
        prob.astype(jnp.bfloat16),
        by_head(g_rows),
        preferred_element_type=jnp.float32,
    )
    return (key_part.reshape(k_rows.shape), value_part.reshape(k_rows.shape))


def tile_back(q_rows, g_rows, k_rows, v_rows, prob, row_delta):
    score_grad = grad_of_scores(g_rows, v_rows, prob, row_delta)
    result = jnp.einsum(
        "hqk,khd->qhd", score_grad, by_head(k_rows), preferred_element_type=jnp.float32
    )
    key_part, value_part = key_terms_of(q_rows, g_rows, k_rows, prob, score_grad)
    return (result.reshape(q_rows.shape), key_part, value_part)


def body(queries, keys, values, grad_out, doc_ids, loss_mask):
    block_rows, width = queries.shape
    seq_index = lax.axis_index(SEQ)
    doc_rows, mask_rows = turned_gather((doc_ids, loss_mask), "head", (0, 0))
    positions = seq_index * block_rows + jnp.arange(block_rows, dtype=jnp.int32)
    catalog = jnp.arange(2 * lax.axis_size(SEQ), dtype=jnp.int32)
    member = doc_rows[:, None] == catalog[None, :]
    local_counts = jnp.sum(jnp.where(member, mask_rows[:, None].astype(jnp.float32), 0.0), axis=0)
    local_first = jnp.min(jnp.where(member, positions[:, None], big_index), axis=0)
    counts = by_axis(local_counts, SEQ)
    firsts = one_axis_at_a_time(local_first, SEQ)
    doc_start = jnp.sum(jnp.where(member, firsts[None, :], 0), axis=1)
    doc_count = jnp.sum(jnp.where(member, counts[None, :], 0.0), axis=1)
    weight = (
        mask_rows.astype(jnp.float32) * block_rows / jnp.maximum(doc_count, float(block_rows // 8))
    )
    remote = []
    carried = (keys, values)
    for distance in range(1, REACH + 1):
        carried = shifted((carried[0], carried[1]), SEQ, 1)
        remote.append(carried)
    key_blocks = [(keys, values)] + remote
    masks = [
        allowed_for(positions, doc_start, positions - distance * block_rows)
        for distance in range(REACH + 1)
    ]
    score_list = [
        tile_scores(queries, key_blocks[distance][0], masks[distance])
        for distance in range(REACH + 1)
    ]
    row_max = reduce(jnp.maximum, [jnp.max(score, axis=2) for score in score_list])
    row_sum = sum((jnp.sum(jnp.exp(score - row_max[..., None]), axis=2) for score in score_list))
    log_total = row_max + jnp.log(row_sum)
    prob_list = [jnp.exp(score - log_total[..., None]) for score in score_list]
    mixed_out = sum(
        (tile_mix(prob_list[distance], key_blocks[distance][1]) for distance in range(REACH + 1))
    )
    attended = mixed_out.astype(jnp.bfloat16).reshape(block_rows, width)
    grad_rows = (weight[:, None] * grad_out.astype(jnp.float32)).astype(jnp.bfloat16)
    row_delta = jnp.sum(
        by_head(grad_rows).astype(jnp.float32) * by_head(attended).astype(jnp.float32), axis=2
    ).T
    terms = [
        tile_back(
            queries,
            grad_rows,
            key_blocks[distance][0],
            key_blocks[distance][1],
            prob_list[distance],
            row_delta,
        )
        for distance in range(REACH + 1)
    ]
    query_total = sum((term[0] for term in terms))
    carried = (terms[REACH][1], terms[REACH][2])
    for distance in range(REACH - 1, -1, -1):
        carried = shifted((for_sending(carried[0]), for_sending(carried[1])), SEQ, -1)
        carried = (carried[0] + terms[distance][1], carried[1] + terms[distance][2])
    return (
        attended,
        query_total.astype(jnp.bfloat16),
        carried[0].astype(jnp.bfloat16),
        carried[1].astype(jnp.bfloat16),
    )


def solution(mesh):
    torus = Mesh(
        mesh.devices.reshape(8, 4, 4, 2, mesh.shape["head"]),
        ("seq_0", "seq_1", "seq_2", "seq_3", "head"),
    )
    in_specs = (
        P(SEQ, "head"),
        P(SEQ, "head"),
        P(SEQ, "head"),
        P(SEQ, "head"),
        P(SEQ_HEAD),
        P(SEQ_HEAD),
    )
    out_specs = (P(SEQ, "head"), P(SEQ, "head"), P(SEQ, "head"), P(SEQ, "head"))
    return jax.shard_map(body, mesh=torus, in_specs=in_specs, out_specs=out_specs, check_vma=False)
```

profile of v0, /device:TPU:255, one launch (start us, length us, event | category | flops | bytes accessed | tf_op | source)
XLA Modules:
  0.0 208.5 jit_solution(2514917617455026863)
XLA Ops:
  0.7 1.2 copy.331
  1.8 8.0 %collective-permute-start = (bf16[128,1024]{0,1:T(8,128)(2,1)S(1)}, bf16[128,1024]{0,1:T(8,128)(2,1)S(1)}, u32[]{:S(2)}, u32[]{:S(2)}) collective-permute-start(bf16[128,1024]{0,1:T(8,128)(2,1)S(1)} %copy.331), channel_id=1, source_target_pairs={{0,2},{2,4},{4,6},{6,8},{8,10},{10,12},{12,14},{14,16},{16,18},{18... | collective-permute-start | bytes 786440 | tf_op jit(solution)/shard_map/ppermute | solution.py:50
  9.9 1.9 collective-permute-start.4
  11.9 0.6 copy-done.31
  12.6 7.0 %all-gather = s32[2,64,2]{1,2,0:T(2,128)S(1)} all-gather(s32[1,64,2]{1,2,0:T(2,128)S(1)} %add_bitcast_fusion), channel_id=1, replica_groups=mesh['seq_0'=8,'seq_1'=4,'seq_2'=4,'seq_3'=2,'head'=2] {'head'}, dimensions={0}, use_global_device_ids=true | all-gather | bytes 1536 | tf_op jit(solution)/shard_map/all_gather | solution.py:25
  19.8 9.4 %pmin.28 = s32[512]{0:T(512)S(1)} all-reduce(s32[512]{0:T(512)S(1)} %select_reduce_fusion.3), channel_id=1, replica_groups=mesh['seq_0'=8,'seq_1'=4,'seq_2'=4,'seq_3'=2,'head'=2] {'seq_0'}, use_global_device_ids=true, to_apply=%region_1.2 | all-reduce | flops 512 | bytes 4096 | tf_op jit(solution)/shard_map/pmin | solution.py:43
  29.1 5.7 %pmin.29 = s32[512]{0:T(512)S(1)} all-reduce(s32[512]{0:T(512)S(1)} %pmin.28), channel_id=1, replica_groups=mesh['seq_0'=8,'seq_1'=4,'seq_2'=4,'seq_3'=2,'head'=2] {'seq_1'}, use_global_device_ids=true, to_apply=%region_2.3 | all-reduce | flops 512 | bytes 4096 | tf_op jit(solution)/shard_map/pmin | solution.py:43
  34.8 4.0 %pmin.30 = s32[512]{0:T(512)S(1)} all-reduce(s32[512]{0:T(512)S(1)} %pmin.29), channel_id=1, replica_groups=mesh['seq_0'=8,'seq_1'=4,'seq_2'=4,'seq_3'=2,'head'=2] {'seq_2'}, use_global_device_ids=true, to_apply=%region_3.4 | all-reduce | flops 512 | bytes 4096 | tf_op jit(solution)/shard_map/pmin | solution.py:43
  38.8 9.3 %pmin.31 = s32[512]{0:T(512)S(1)} all-reduce(s32[512]{0:T(512)S(1)} %pmin.30), channel_id=1, replica_groups=mesh['seq_0'=8,'seq_1'=4,'seq_2'=4,'seq_3'=2,'head'=2] {'seq_3'}, use_global_device_ids=true, to_apply=%region_4.5 | all-reduce | flops 512 | bytes 4096 | tf_op jit(solution)/shard_map/pmin | solution.py:43
  48.8 10.6 %psum.28 = f32[512]{0:T(512)S(1)} all-reduce(f32[512]{0:T(512)S(1)} %select_reduce_fusion.1), channel_id=1, replica_groups=mesh['seq_0'=8,'seq_1'=4,'seq_2'=4,'seq_3'=2,'head'=2] {'seq_0'}, use_global_device_ids=true, to_apply=%region_17.18 | all-reduce | flops 512 | bytes 4096 | tf_op jit(solution)/shard_map/psum | solution.py:37
  59.4 6.3 %psum.29 = f32[512]{0:T(512)S(1)} all-reduce(f32[512]{0:T(512)S(1)} %psum.28), channel_id=1, replica_groups=mesh['seq_0'=8,'seq_1'=4,'seq_2'=4,'seq_3'=2,'head'=2] {'seq_1'}, use_global_device_ids=true, to_apply=%region_18.19 | all-reduce | flops 512 | bytes 4096 | tf_op jit(solution)/shard_map/psum | solution.py:37
  65.6 7.3 %psum.30 = f32[512]{0:T(512)S(1)} all-reduce(f32[512]{0:T(512)S(1)} %psum.29), channel_id=1, replica_groups=mesh['seq_0'=8,'seq_1'=4,'seq_2'=4,'seq_3'=2,'head'=2] {'seq_2'}, use_global_device_ids=true, to_apply=%region_19.20 | all-reduce | flops 512 | bytes 4096 | tf_op jit(solution)/shard_map/psum | solution.py:37
  72.9 10.1 %psum.31 = f32[512]{0:T(512)S(1)} all-reduce(f32[512]{0:T(512)S(1)} %psum.30), channel_id=1, replica_groups=mesh['seq_0'=8,'seq_1'=4,'seq_2'=4,'seq_3'=2,'head'=2] {'seq_3'}, use_global_device_ids=true, to_apply=%region_20.21 | all-reduce | flops 512 | bytes 4096 | tf_op jit(solution)/shard_map/psum | solution.py:37
  83.4 10.3 %collective-permute-start.1 = (bf16[128,1024]{0,1:T(8,128)(2,1)S(1)}, bf16[128,1024]{0,1:T(8,128)(2,1)S(1)}, u32[]{:S(2)}, u32[]{:S(2)}) collective-permute-start(bf16[128,1024]{0,1:T(8,128)(2,1)S(1)} %collective-permute-done), channel_id=1, source_target_pairs={{0,2},{2,4},{4,6},{6,8},{8,10},{10,12},{12,14},{14,16},{16,18},{18... | collective-permute-start | bytes 786440 | tf_op jit(solution)/shard_map/ppermute | solution.py:50
  93.8 2.1 collective-permute-start.5
  95.9 1.0 collective-permute-done.1
  96.9 10.4 %collective-permute-start.2 = (bf16[128,1024]{0,1:T(8,128)(2,1)S(1)}, bf16[128,1024]{0,1:T(8,128)(2,1)}, u32[]{:S(2)}, u32[]{:S(2)}) collective-permute-start(bf16[128,1024]{0,1:T(8,128)(2,1)S(1)} %collective-permute-done.1), channel_id=1, source_target_pairs={{0,2},{2,4},{4,6},{6,8},{8,10},{10,12},{12,14},{14,16},{16,18},{18... | collective-permute-start | bytes 786440 | tf_op jit(solution)/shard_map/ppermute | solution.py:50
  107.6 2.5 %collective-permute-start.6 = (bf16[128,1024]{1,0:T(8,128)(2,1)S(1)}, bf16[128,1024]{1,0:T(8,128)(2,1)}, u32[]{:S(2)}, u32[]{:S(2)}) collective-permute-start(bf16[128,1024]{1,0:T(8,128)(2,1)S(1)} %collective-permute-done.5), channel_id=1, source_target_pairs={{0,2},{2,4},{4,6},{6,8},{8,10},{10,12},{12,14},{14,16},{16,18},{18... | collective-permute-start | bytes 786440 | tf_op jit(solution)/shard_map/ppermute | solution.py:50
  110.6 10.5 %collective-permute-start.3 = (bf16[128,1024]{0,1:T(8,128)(2,1)}, bf16[128,1024]{0,1:T(8,128)(2,1)S(1)}, u32[]{:S(2)}, u32[]{:S(2)}) collective-permute-start(bf16[128,1024]{0,1:T(8,128)(2,1)} %collective-permute-done.2), channel_id=1, source_target_pairs={{0,2},{2,4},{4,6},{6,8},{8,10},{10,12},{12,14},{14,16},{16,18},{18... | collective-permute-start | bytes 786440 | tf_op jit(solution)/shard_map/ppermute | solution.py:50
  121.4 0.8 copy.237
  122.3 1.8 copy.239
  124.1 1.9 collective-permute-start.7
  126.0 1.2 fusion.48
  127.3 0.7 copy-done.23
  128.0 1.2 fusion.47
  130.7 0.7 copy-done
  131.6 0.7 copy-done.2
  132.4 1.0 convolution_add_fusion.5
  133.4 1.8 copy.241
  135.2 2.1 %multiply_reduce_fusion = (f32[128,8]{0,1:T(8,128)S(1)}, bf16[8,128,128]{1,2,0:T(8,128)(2,1)}) fusion(bf16[128,1024]{0,1:T(8,128)(2,1)S(1)} %copy.243, f32[8,128,128]{1,2,0:T(8,128)} %convolution_add_fusion.5, bf16[128,8,128]{0,2,1:T(8,128)(2,1)} %bitcast.152, f32[8,128,128]{1,2,0:T(8,128)S(1)} %get-tuple-element.33, f32[8,128]{1,0:T(8,128)S(1)} %log_add_fusion), kind=kOutput, calls=%fused_computation.50 | convolution fusion | flops 34601984 | bytes 1843200 | tf_op jit(solution)/shard_map/hqk,khd->qhd/dot_general | solution.py:80
  137.9 0.7 copy-done.1
  138.9 0.7 copy-done.3
  140.0 0.7 copy-done.4
  141.0 1.1 fusion.43
  142.1 1.1 fusion.40
  143.2 1.1 fusion.37
  144.3 1.1 fusion.34
  146.0 0.6 copy-done.26
  146.9 0.7 copy-done.28
  147.8 1.2 convolution_add_fusion.1
  149.4 2.4 %collective-permute-start.8 = (bf16[128,1024]{1,0:T(8,128)(2,1)S(1)}, bf16[128,1024]{1,0:T(8,128)(2,1)S(1)}, u32[]{:S(2)}, u32[]{:S(2)}) collective-permute-start(bf16[128,1024]{1,0:T(8,128)(2,1)S(1)} %copy.267), channel_id=1, source_target_pairs={{2,0},{4,2},{6,4},{8,6},{10,8},{12,10},{14,12},{16,14},{18,16},{20... | collective-permute-start | bytes 786440 | tf_op jit(solution)/shard_map/ppermute | solution.py:50
  152.3 1.9 collective-permute-start.12
  154.8 0.8 copy-done.18
  155.8 7.3 %collective-permute-done.8 = bf16[128,1024]{1,0:T(8,128)(2,1)S(1)} collective-permute-done((bf16[128,1024]{1,0:T(8,128)(2,1)S(1)}, bf16[128,1024]{1,0:T(8,128)(2,1)S(1)}, u32[]{:S(2)}, u32[]{:S(2)}) %collective-permute-start.8) | collective-permute-done | bytes 262176 | tf_op jit(solution)/shard_map/ppermute | solution.py:50
  163.2 2.1 collective-permute-start.9
  165.3 0.8 collective-permute-done.12
  166.1 1.9 collective-permute-start.13
  168.6 0.8 copy-done.17
  169.6 7.5 %collective-permute-done.9 = bf16[128,1024]{1,0:T(8,128)(2,1)S(1)} collective-permute-done((bf16[128,1024]{1,0:T(8,128)(2,1)S(1)}, bf16[128,1024]{1,0:T(8,128)(2,1)S(1)}, u32[]{:S(2)}, u32[]{:S(2)}) %collective-permute-start.9) | collective-permute-done | bytes 262176 | tf_op jit(solution)/shard_map/ppermute | solution.py:50
  177.1 2.1 collective-permute-start.10
  179.2 0.7 collective-permute-done.13
  179.9 1.9 collective-permute-start.14
  182.4 0.8 copy-done.16
  183.4 7.6 %collective-permute-done.10 = bf16[128,1024]{1,0:T(8,128)(2,1)S(1)} collective-permute-done((bf16[128,1024]{1,0:T(8,128)(2,1)S(1)}, bf16[128,1024]{1,0:T(8,128)(2,1)S(1)}, u32[]{:S(2)}, u32[]{:S(2)}) %collective-permute-start.10) | collective-permute-done | bytes 262176 | tf_op jit(solution)/shard_map/ppermute | solution.py:50
  191.0 2.1 collective-permute-start.11
  193.1 0.7 collective-permute-done.14
  193.9 2.1 collective-permute-start.15
  196.2 0.9 copy.290
  197.1 0.8 copy.291
  198.1 0.8 copy-done.15
  199.2 5.7 %collective-permute-done.11 = bf16[128,1024]{1,0:T(8,128)(2,1)S(1)} collective-permute-done((bf16[128,1024]{1,0:T(8,128)(2,1)S(1)}, bf16[128,1024]{1,0:T(8,128)(2,1)S(1)}, u32[]{:S(2)}, u32[]{:S(2)}) %collective-permute-start.11) | collective-permute-done | bytes 262176 | tf_op jit(solution)/shard_map/ppermute | solution.py:50
  204.9 0.8 add_convert_fusion.4
  205.6 2.0 collective-permute-done.15
  207.7 0.8 add_convert_fusion
  (117 shorter events, 10.4 us)
Async XLA Ops:
  0.6 9.3 %copy-start.19 = (bf16[128,1024]{1,0:T(8,128)(2,1)S(1)}, bf16[128,1024]{1,0:T(8,128)(2,1)}, u32[]{:S(2)}) copy-start(bf16[128,1024]{1,0:T(8,128)(2,1)} %param.8) | copy-start | bytes 786436
  0.6 48.0 %copy-start.30 = (bf16[128,1024]{1,0:T(8,128)(2,1)S(1)}, bf16[128,1024]{1,0:T(8,128)(2,1)}, u32[]{:S(2)}) copy-start(bf16[128,1024]{1,0:T(8,128)(2,1)} %param.6) | copy-start | bytes 786436
  1.8 81.2 %copy-start.13 = (bf16[128,1024]{0,1:T(8,128)(2,1)}, bf16[128,1024]{0,1:T(8,128)(2,1)S(1)}, u32[]{:S(2)}) copy-start(bf16[128,1024]{0,1:T(8,128)(2,1)S(1)} %copy.331) | copy-start | bytes 786436
  1.8 81.5 %collective-permute-start = (bf16[128,1024]{0,1:T(8,128)(2,1)S(1)}, bf16[128,1024]{0,1:T(8,128)(2,1)S(1)}, u32[]{:S(2)}, u32[]{:S(2)}) collective-permute-start(bf16[128,1024]{0,1:T(8,128)(2,1)S(1)} %copy.331), channel_id=1, source_target_pairs={{0,2},{2,4},{4,6},{6,8},{8,10},{10,12},{12,14},{14,16},{16,18},{18... | collective-permute-start | bytes 786440 | tf_op jit(solution)/shard_map/ppermute | solution.py:50
  9.9 83.9 %collective-permute-start.4 = (bf16[128,1024]{1,0:T(8,128)(2,1)S(1)}, bf16[128,1024]{1,0:T(8,128)(2,1)S(1)}, u32[]{:S(2)}, u32[]{:S(2)}) collective-permute-start(bf16[128,1024]{1,0:T(8,128)(2,1)S(1)} %copy-done.19), channel_id=1, source_target_pairs={{0,2},{2,4},{4,6},{6,8},{8,10},{10,12},{12,14},{14,16},{16,18},{18... | collective-permute-start | bytes 786440 | tf_op jit(solution)/shard_map/ppermute | solution.py:50
  11.9 0.7 copy-start.31
  11.9 0.7 copy-start.32
  83.0 24.3 %copy-start.29 = (bf16[128,1024]{1,0:T(8,128)(2,1)S(1)}, bf16[128,1024]{1,0:T(8,128)(2,1)}, u32[]{:S(2)}) copy-start(bf16[128,1024]{1,0:T(8,128)(2,1)} %param.9) | copy-start | bytes 786436
  83.3 26.8 %copy-start.25 = (bf16[128,1024]{0,1:T(8,128)(2,1)}, bf16[128,1024]{0,1:T(8,128)(2,1)S(1)}, u32[]{:S(2)}) copy-start(bf16[128,1024]{0,1:T(8,128)(2,1)S(1)} %collective-permute-done) | copy-start | bytes 786436
  83.4 13.6 %collective-permute-start.1 = (bf16[128,1024]{0,1:T(8,128)(2,1)S(1)}, bf16[128,1024]{0,1:T(8,128)(2,1)S(1)}, u32[]{:S(2)}, u32[]{:S(2)}) collective-permute-start(bf16[128,1024]{0,1:T(8,128)(2,1)S(1)} %collective-permute-done), channel_id=1, source_target_pairs={{0,2},{2,4},{4,6},{6,8},{8,10},{10,12},{12,14},{14,16},{16,18},{18... | collective-permute-start | bytes 786440 | tf_op jit(solution)/shard_map/ppermute | solution.py:50
  93.8 13.8 %collective-permute-start.5 = (bf16[128,1024]{1,0:T(8,128)(2,1)S(1)}, bf16[128,1024]{1,0:T(8,128)(2,1)S(1)}, u32[]{:S(2)}, u32[]{:S(2)}) collective-permute-start(bf16[128,1024]{1,0:T(8,128)(2,1)S(1)} %collective-permute-done.4), channel_id=1, source_target_pairs={{0,2},{2,4},{4,6},{6,8},{8,10},{10,12},{12,14},{14,16},{16,18},{18... | collective-permute-start | bytes 786440 | tf_op jit(solution)/shard_map/ppermute | solution.py:50
  96.9 24.2 %copy-start.27 = (bf16[128,1024]{0,1:T(8,128)(2,1)}, bf16[128,1024]{0,1:T(8,128)(2,1)S(1)}, u32[]{:S(2)}) copy-start(bf16[128,1024]{0,1:T(8,128)(2,1)S(1)} %collective-permute-done.1) | copy-start | bytes 786436
  96.9 13.7 %collective-permute-start.2 = (bf16[128,1024]{0,1:T(8,128)(2,1)S(1)}, bf16[128,1024]{0,1:T(8,128)(2,1)}, u32[]{:S(2)}, u32[]{:S(2)}) collective-permute-start(bf16[128,1024]{0,1:T(8,128)(2,1)S(1)} %collective-permute-done.1), channel_id=1, source_target_pairs={{0,2},{2,4},{4,6},{6,8},{8,10},{10,12},{12,14},{14,16},{16,18},{18... | collective-permute-start | bytes 786440 | tf_op jit(solution)/shard_map/ppermute | solution.py:50
  107.6 14.6 %collective-permute-start.6 = (bf16[128,1024]{1,0:T(8,128)(2,1)S(1)}, bf16[128,1024]{1,0:T(8,128)(2,1)}, u32[]{:S(2)}, u32[]{:S(2)}) collective-permute-start(bf16[128,1024]{1,0:T(8,128)(2,1)S(1)} %collective-permute-done.5), channel_id=1, source_target_pairs={{0,2},{2,4},{4,6},{6,8},{8,10},{10,12},{12,14},{14,16},{16,18},{18... | collective-permute-start | bytes 786440 | tf_op jit(solution)/shard_map/ppermute | solution.py:50
  110.6 16.6 %collective-permute-start.3 = (bf16[128,1024]{0,1:T(8,128)(2,1)}, bf16[128,1024]{0,1:T(8,128)(2,1)S(1)}, u32[]{:S(2)}, u32[]{:S(2)}) collective-permute-start(bf16[128,1024]{0,1:T(8,128)(2,1)} %collective-permute-done.2), channel_id=1, source_target_pairs={{0,2},{2,4},{4,6},{6,8},{8,10},{10,12},{12,14},{14,16},{16,18},{18... | collective-permute-start | bytes 786440 | tf_op jit(solution)/shard_map/ppermute | solution.py:50
  124.1 9.3 %collective-permute-start.7 = (bf16[128,1024]{1,0:T(8,128)(2,1)}, bf16[128,1024]{1,0:T(8,128)(2,1)}, u32[]{:S(2)}, u32[]{:S(2)}) collective-permute-start(bf16[128,1024]{1,0:T(8,128)(2,1)} %collective-permute-done.6), channel_id=1, source_target_pairs={{0,2},{2,4},{4,6},{6,8},{8,10},{10,12},{12,14},{14,16},{16,18},{18... | collective-permute-start | bytes 786440 | tf_op jit(solution)/shard_map/ppermute | solution.py:50
  127.2 0.7 copy-start.23
  129.2 1.0 copy-start.20
  130.4 1.0 copy-start
  131.4 0.9 copy-start.2
  135.2 2.1 %copy-start.21 = (bf16[128,1024]{1,0:T(8,128)(2,1)S(1)}, bf16[128,1024]{1,0:T(8,128)(2,1)}, u32[]{:S(2)}) copy-start(bf16[128,1024]{1,0:T(8,128)(2,1)} %param.8) | copy-start | bytes 786436
  137.5 7.9 %copy-start.5 = (bf16[8,128,128]{1,2,0:T(8,128)(2,1)}, bf16[8,128,128]{1,2,0:T(8,128)(2,1)S(1)}, u32[]{:S(2)}) copy-start(bf16[8,128,128]{1,2,0:T(8,128)(2,1)S(1)} %fusion.19) | copy-start | bytes 786436
  137.6 1.0 copy-start.1
  138.6 7.4 %copy-start.7 = (bf16[8,128,128]{1,2,0:T(8,128)(2,1)}, bf16[8,128,128]{1,2,0:T(8,128)(2,1)S(1)}, u32[]{:S(2)}) copy-start(bf16[8,128,128]{1,2,0:T(8,128)(2,1)S(1)} %fusion.15) | copy-start | bytes 786436
  138.6 1.0 copy-start.3
  139.7 7.2 %copy-start.9 = (bf16[8,128,128]{1,2,0:T(8,128)(2,1)}, bf16[8,128,128]{1,2,0:T(8,128)(2,1)S(1)}, u32[]{:S(2)}) copy-start(bf16[8,128,128]{1,2,0:T(8,128)(2,1)S(1)} %fusion.16) | copy-start | bytes 786436
  139.7 1.0 copy-start.4
  140.7 7.1 %copy-start.11 = (bf16[8,128,128]{1,2,0:T(8,128)(2,1)}, bf16[8,128,128]{1,2,0:T(8,128)(2,1)S(1)}, u32[]{:S(2)}) copy-start(bf16[8,128,128]{1,2,0:T(8,128)(2,1)S(1)} %fusion.17) | copy-start | bytes 786436
  144.3 1.1 copy-start.14
  145.7 1.0 copy-start.26
  146.6 0.9 copy-start.28
  147.8 1.2 copy-start.24
  149.4 13.7 %collective-permute-start.8 = (bf16[128,1024]{1,0:T(8,128)(2,1)S(1)}, bf16[128,1024]{1,0:T(8,128)(2,1)S(1)}, u32[]{:S(2)}, u32[]{:S(2)}) collective-permute-start(bf16[128,1024]{1,0:T(8,128)(2,1)S(1)} %copy.267), channel_id=1, source_target_pairs={{2,0},{4,2},{6,4},{8,6},{10,8},{12,10},{14,12},{16,14},{18,16},{20... | collective-permute-start | bytes 786440 | tf_op jit(solution)/shard_map/ppermute | solution.py:50
  152.2 2.1 %copy-start.12 = (bf16[8,128,128]{1,2,0:T(8,128)(2,1)S(1)}, bf16[8,128,128]{1,2,0:T(8,128)(2,1)}, u32[]{:S(2)}) copy-start(bf16[8,128,128]{1,2,0:T(8,128)(2,1)} %copy-done.11) | copy-start | bytes 786436
  152.3 13.7 %collective-permute-start.12 = (bf16[128,1024]{1,0:T(8,128)(2,1)S(1)}, bf16[128,1024]{1,0:T(8,128)(2,1)S(1)}, u32[]{:S(2)}, u32[]{:S(2)}) collective-permute-start(bf16[128,1024]{1,0:T(8,128)(2,1)S(1)} %copy.281), channel_id=1, source_target_pairs={{2,0},{4,2},{6,4},{8,6},{10,8},{12,10},{14,12},{16,14},{18,16},{20... | collective-permute-start | bytes 786440 | tf_op jit(solution)/shard_map/ppermute | solution.py:50
  154.6 1.0 copy-start.18
  163.2 4.8 %copy-start.10 = (bf16[8,128,128]{1,2,0:T(8,128)(2,1)S(1)}, bf16[8,128,128]{1,2,0:T(8,128)(2,1)}, u32[]{:S(2)}) copy-start(bf16[8,128,128]{1,2,0:T(8,128)(2,1)} %copy-done.9) | copy-start | bytes 786436
  163.2 13.8 %collective-permute-start.9 = (bf16[128,1024]{1,0:T(8,128)(2,1)S(1)}, bf16[128,1024]{1,0:T(8,128)(2,1)S(1)}, u32[]{:S(2)}, u32[]{:S(2)}) collective-permute-start(bf16[128,1024]{1,0:T(8,128)(2,1)S(1)} %add_convert_fusion.7), channel_id=1, source_target_pairs={{2,0},{4,2},{6,4},{8,6},{10,8},{12,10},{14,12},{16,14},{18,16},{20... | collective-permute-start | bytes 786440 | tf_op jit(solution)/shard_map/ppermute | solution.py:50
  166.1 13.8 %collective-permute-start.13 = (bf16[128,1024]{1,0:T(8,128)(2,1)S(1)}, bf16[128,1024]{1,0:T(8,128)(2,1)S(1)}, u32[]{:S(2)}, u32[]{:S(2)}) collective-permute-start(bf16[128,1024]{1,0:T(8,128)(2,1)S(1)} %add_convert_fusion.3), channel_id=1, source_target_pairs={{2,0},{4,2},{6,4},{8,6},{10,8},{12,10},{14,12},{16,14},{18,16},{20... | collective-permute-start | bytes 786440 | tf_op jit(solution)/shard_map/ppermute | solution.py:50
  168.3 1.0 copy-start.17
  177.1 4.7 %copy-start.8 = (bf16[8,128,128]{1,2,0:T(8,128)(2,1)S(1)}, bf16[8,128,128]{1,2,0:T(8,128)(2,1)}, u32[]{:S(2)}) copy-start(bf16[8,128,128]{1,2,0:T(8,128)(2,1)} %copy-done.7) | copy-start | bytes 786436
  177.1 13.8 %collective-permute-start.10 = (bf16[128,1024]{1,0:T(8,128)(2,1)S(1)}, bf16[128,1024]{1,0:T(8,128)(2,1)S(1)}, u32[]{:S(2)}, u32[]{:S(2)}) collective-permute-start(bf16[128,1024]{1,0:T(8,128)(2,1)S(1)} %add_convert_fusion.6), channel_id=1, source_target_pairs={{2,0},{4,2},{6,4},{8,6},{10,8},{12,10},{14,12},{16,14},{18,16},{20... | collective-permute-start | bytes 786440 | tf_op jit(solution)/shard_map/ppermute | solution.py:50
  179.9 13.9 %collective-permute-start.14 = (bf16[128,1024]{1,0:T(8,128)(2,1)S(1)}, bf16[128,1024]{1,0:T(8,128)(2,1)S(1)}, u32[]{:S(2)}, u32[]{:S(2)}) collective-permute-start(bf16[128,1024]{1,0:T(8,128)(2,1)S(1)} %add_convert_fusion.2), channel_id=1, source_target_pairs={{2,0},{4,2},{6,4},{8,6},{10,8},{12,10},{14,12},{16,14},{18,16},{20... | collective-permute-start | bytes 786440 | tf_op jit(solution)/shard_map/ppermute | solution.py:50
  182.2 1.0 copy-start.16
  191.0 4.9 %copy-start.6 = (bf16[8,128,128]{1,2,0:T(8,128)(2,1)S(1)}, bf16[8,128,128]{1,2,0:T(8,128)(2,1)}, u32[]{:S(2)}) copy-start(bf16[8,128,128]{1,2,0:T(8,128)(2,1)} %copy-done.5) | copy-start | bytes 786436
  191.0 13.8 %collective-permute-start.11 = (bf16[128,1024]{1,0:T(8,128)(2,1)S(1)}, bf16[128,1024]{1,0:T(8,128)(2,1)S(1)}, u32[]{:S(2)}, u32[]{:S(2)}) collective-permute-start(bf16[128,1024]{1,0:T(8,128)(2,1)S(1)} %add_convert_fusion.5), channel_id=1, source_target_pairs={{2,0},{4,2},{6,4},{8,6},{10,8},{12,10},{14,12},{16,14},{18,16},{20... | collective-permute-start | bytes 786440 | tf_op jit(solution)/shard_map/ppermute | solution.py:50
  193.8 2.4 %copy-start.22 = (bf16[8,128,128]{1,2,0:T(8,128)(2,1)S(1)}, bf16[8,128,128]{1,2,0:T(8,128)(2,1)}, u32[]{:S(2)}) copy-start(bf16[8,128,128]{1,2,0:T(8,128)(2,1)} %get-tuple-element.43) | copy-start | bytes 786436
  193.9 13.8 %collective-permute-start.15 = (bf16[128,1024]{1,0:T(8,128)(2,1)S(1)}, bf16[128,1024]{1,0:T(8,128)(2,1)S(1)}, u32[]{:S(2)}, u32[]{:S(2)}) collective-permute-start(bf16[128,1024]{1,0:T(8,128)(2,1)S(1)} %add_convert_fusion.1), channel_id=1, source_target_pairs={{2,0},{4,2},{6,4},{8,6},{10,8},{12,10},{14,12},{16,14},{18,16},{20... | collective-permute-start | bytes 786440 | tf_op jit(solution)/shard_map/ppermute | solution.py:50
  197.9 1.0 copy-start.15
where the time goes:
time: 210 us; the launch traced here: 208 us
  blocking collectives  69.6 us (33%)
  starting transfers between devices  64 us (30%)
  waiting for transfers between devices  33.2 us (16%)
  local copies, waits for them, and re-layouts  20 us (10%)
  matrix products  17 us (8%)
  other arithmetic  3.2 us (2%)
    ppermute x16, starting transfers between devices, shifted(): return lax.ppermute(block, axis, route)  64 us
    psum x4, blocking collectives, by_axis(): value = lax.psum(value, axis)  34.3 us
    ppermute x16, waiting for transfers between devices, shifted(): return lax.ppermute(block, axis, route)  33.2 us
    pmin x4, blocking collectives, one_axis_at_a_time(): value = lax.pmin(value, axis)  28.4 us
    unnamed x69, local copies, waits for them, and re-layouts  12 us
    all_gather x1, blocking collectives, turned_gather(): out = lax.all_gather(both, axis, axis=0, tiled=True)  6.99 us
    dot_general x5, matrix products, key_terms_of(): jnp.einsum('hqk,qhd->khd', prob.astype(jnp.bfloat16), by_head(g_rows), pr...  4.77 us
    ppermute x4, local copies, waits for them, and re-layouts, shifted(): return lax.ppermute(block, axis, route)  4.59 us
  transfers between devices with their start and end apart: 16, of which 9 were waited for; matrix products, arithmetic and copies ran while one was open for 8% of the time, Pallas kernels for 0%

commit v1 on v0

v1 whole, which is shorter than its diff:
```python
import functools
import math

import jax
import jax.numpy as jnp
from jax import lax
from jax.experimental import pallas as pl
from jax.experimental.pallas import tpu as pltpu
from jax.sharding import PartitionSpec as P

HEAD_DIM = 128
MASKED = -1e30
SCALE = 1.0 / math.sqrt(HEAD_DIM)
MESH = pl.DeviceIdType.MESH
NN = (((1,), (0,)), ((), ()))
NT = (((1,), (1,)), ((), ()))
TN = (((0,), (0,)), ((), ()))


def dot(a, b, dims):
    return lax.dot_general(a, b, dims, preferred_element_type=jnp.float32)


def kernel(
    n_chip,
    rows,
    heads,
    q_in,
    k_in,
    v_in,
    g_in,
    ids_in,
    mask_in,
    o_out,
    qg_out,
    kg_out,
    vg_out,
    own,
    near,
    far,
    meta_mine,
    meta,
    bias,
    weight,
    outs,
    outs_other,
    own_terms,
    near_terms,
    other_send,
    other_got,
    far_send,
    far_got,
    near_send,
    near_got,
    result,
    load_sem,
    own_ssem,
    own_rsem,
    near_ssem,
    near_rsem,
    far_ssem,
    far_rsem,
    meta_ssem,
    meta_rsem,
    outs_ssem,
    outs_rsem,
    store_sem,
    other_ssem,
    other_rsem,
    fterm_ssem,
    fterm_rsem,
    nterm_ssem,
    nterm_rsem,
):
    D = HEAD_DIM
    me = lax.axis_index("seq")
    hd = lax.axis_index("head")
    chip, core = me // 2, lax.rem(me, 2)
    right, left = lax.rem(chip + 1, n_chip), lax.rem(chip + n_chip - 1, n_chip)
    ins = (q_in, k_in, v_in, g_in)

    def at_chip(offset):
        return lax.rem(chip + n_chip + offset, n_chip)

    def half(which):
        return pl.ds(pl.multiple_of(which * rows, rows), rows)

    def columns(which, h):
        return pl.ds(pl.multiple_of((which * heads + h) * D, D), D)

    def remote(src, dst, ssem, rsem, to_chip, to_core, to_hd=None):
        return pltpu.make_async_remote_copy(
            src_ref=src,
            dst_ref=dst,
            send_sem=ssem,
            recv_sem=rsem,
            device_id=(to_chip * 2 + to_core, hd if to_hd is None else to_hd),
            device_id_type=MESH,
        )

    def load(t, h):
        return pltpu.make_async_copy(
            ins[t].at[:, columns(core, h)], own.at[t, h, half(core)], load_sem.at[t, h]
        )

    for t in range(4):
        for h in range(heads):
            load(t, h).start()

    peers = []
    for offset in (-2, -1, 0, 1, 2):
        for c in range(2):
            for d in range(2):
                if offset == 0:
                    if c == 0 and d == 0:
                        continue
                    peers.append((0, lax.rem(core + c, 2), lax.rem(hd + d, 2)))
                else:
                    peers.append((offset, c, d))

    barrier = pltpu.get_barrier_semaphore()
    for offset, c, d in peers:
        pl.semaphore_signal(
            barrier, inc=1, device_id=(at_chip(offset) * 2 + c, d), device_id_type=MESH
        )

    packed = ids_in[...] * 2 + mask_in[...]
    wide = jnp.concatenate([packed, packed], axis=1)
    lane = lax.broadcasted_iota(jnp.int32, (1, 128), 1)
    wide = jnp.where((lane // 64) == hd, wide, 0)
    meta_mine[...] = wide
    meta[8 + core * 2 + hd] = wide

    pl.semaphore_wait(barrier, len(peers))

    def near_copy(h, c, t):
        return remote(
            ins[1 + t].at[:, columns(c, h)],
            near.at[t, h, half(core)],
            near_ssem.at[h, c, t],
            near_rsem.at[h, core, t],
            right,
            c,
        )

    def near_arrival(h, c, t):
        return remote(
            near.at[t, h, half(c)], near.at[t, h, half(c)], near_ssem.at[h, c, t], near_rsem.at[h, c, t], right, core
        )

    def far_copy(h, t):
        return remote(near.at[t, h], far.at[t, h], far_ssem.at[h, t], far_rsem.at[h, t], right, core)

    def send_near(h):
        for t in range(2):
            for c in range(2):
                near_copy(h, c, t).start()

    def relay(h):
        for c in range(2):
            for t in range(2):
                near_arrival(h, c, t).wait_recv()
        for t in range(2):
            far_copy(h, t).start()

    def own_copy(t, h):
        return remote(
            ins[t].at[:, columns(1 - core, h)],
            own.at[t, h, half(core)],
            own_ssem.at[t, h],
            own_rsem.at[t, h],
            chip,
            1 - core,
        )

    def meta_copy(peer):
        offset, c, d = peer
        return remote(
            meta_mine,
            meta.at[(2 - offset) * 4 + core * 2 + hd],
            meta_ssem.at[(2 + offset) * 4 + c * 2 + d],
            meta_rsem.at[(2 - offset) * 4 + core * 2 + hd],
            at_chip(offset),
            c,
            d,
        )

    def meta_arrival(peer):
        offset, c, d = peer
        place = (2 + offset) * 4 + c * 2 + d
        return remote(meta_mine, meta.at[place], meta_ssem.at[place], meta_rsem.at[place], at_chip(offset), c, d)

    send_near(0)
    for peer in peers:
        meta_copy(peer).start()
    for h in range(heads):
        for t in range(4):
            own_copy(t, h).start()
    send_near(1)

    relay(0)
    send_near(2)

    for peer in peers:
        meta_arrival(peer).wait_recv()

    def row_of(place):
        return meta[4 * (place // 2) + 2 * (place % 2)] + meta[4 * (place // 2) + 2 * (place % 2) + 1]

    key_rows = [row_of(place) for place in range(10)]
    key_docs = [r // 2 for r in key_rows]
    key_loss = [(r - 2 * (r // 2)).astype(jnp.float32) for r in key_rows]
    for part in range(2):
        mine = jnp.broadcast_to(key_rows[4 + part].astype(jnp.float32), (128, 128)).T.astype(jnp.int32)
        doc_q = mine // 2
        loss_q = (mine - 2 * doc_q).astype(jnp.float32)
        count = jnp.zeros((128, 128), jnp.float32)
        for place in range(10):
            same = doc_q == key_docs[place]
            count = count + jnp.where(same, key_loss[place], 0.0)
            if place < 6:
                if place == 4 + part:
                    q_at = lax.broadcasted_iota(jnp.int32, (128, 128), 0)
                    k_at = lax.broadcasted_iota(jnp.int32, (128, 128), 1)
                    same = jnp.logical_and(same, k_at <= q_at)
                if place > 4 + part:
                    block = jnp.full((128, 128), MASKED, jnp.float32)
                else:
                    block = jnp.where(same, 0.0, MASKED)
                bias[part * 128 : part * 128 + 128, place * 128 : place * 128 + 128] = block
        count = jnp.sum(count, axis=1, keepdims=True)
        weight[part * 128 : part * 128 + 128, :] = loss_q * float(rows) / jnp.maximum(count, float(rows // 8))

    for t in range(4):
        for h in range(heads):
            load(t, h).wait()
            remote(
                own.at[t, h, half(1 - core)],
                own.at[t, h, half(1 - core)],
                own_ssem.at[t, h],
                own_rsem.at[t, h],
                chip,
                1 - core,
            ).wait_recv()

    relay(1)
    send_near(3)

    def outs_copy(t, h):
        return remote(
            outs.at[t, h, half(1 - core)],
            outs_other.at[t, h],
            outs_ssem.at[t, h],
            outs_rsem.at[t, h],
            chip,
            1 - core,
        )

    def other_copy(t, h):
        return remote(
            other_send.at[t, h], other_got.at[t, h], other_ssem.at[t, h], other_rsem.at[t, h], chip, 1 - core
        )

    def fterm_copy(t, h):
        return remote(far_send.at[t, h], far_got.at[t, h], fterm_ssem.at[t, h], fterm_rsem.at[t, h], left, core)

    def nterm_copy(t, h, c):
        return remote(
            near_send.at[t, h, half(c)],
            near_got.at[t, core * heads + h],
            nterm_ssem.at[t, h, c],
            nterm_rsem.at[t, core * heads + h],
            left,
            c,
        )

    def store(t, h):
        return pltpu.make_async_copy(
            outs.at[t, h, half(core)], (o_out, qg_out)[t].at[:, columns(core, h)], store_sem.at[t, core * heads + h]
        )

    def store_other(t, h):
        return pltpu.make_async_copy(
            outs_other.at[t, h],
            (o_out, qg_out)[t].at[:, columns(1 - core, h)],
            store_sem.at[t, (1 - core) * heads + h],
        )

    def result_copy(t, j):
        return pltpu.make_async_copy(
            result.at[t, j], (kg_out, vg_out)[t].at[:, pl.ds(j * D, D)], store_sem.at[2 + t, j]
        )

    def send_nterm(h):
        for t in range(2):
            fterm_copy(t, h).wait_recv()
        for t in range(2):
            near_send[t, h] = (near_terms[t, h] + far_got[t, h].astype(jnp.float32)).astype(jnp.bfloat16)
        for t in range(2):
            for c in range(2):
                nterm_copy(t, h, c).start()

    def one_head(h, carry):
        for t in range(2):
            far_copy(h, t).wait_recv()
        q, g = own[0, h], (weight[...] * own[3, h].astype(jnp.float32)).astype(jnp.bfloat16)
        ks = (far[0, h], near[0, h], own[1, h])
        vs = (far[1, h], near[1, h], own[2, h])
        width = 2 * rows
        scores = [dot(q, ks[b], NT) * SCALE + bias[:, b * width : (b + 1) * width] for b in range(3)]
        top = jnp.max(functools.reduce(jnp.maximum, scores), axis=1, keepdims=True)
        prob = [jnp.exp(s - top) for s in scores]
        total = jnp.sum(prob[0] + prob[1] + prob[2], axis=1, keepdims=True)
        inverse = 1.0 / total
        prob = [p * inverse for p in prob]
        prob_half = [p.astype(jnp.bfloat16) for p in prob]
        attended = sum(dot(prob_half[b], vs[b], NN) for b in range(3)).astype(jnp.bfloat16)
        outs[0, h] = attended
        delta = jnp.sum(g.astype(jnp.float32) * attended.astype(jnp.float32), axis=1, keepdims=True)
        score_grad = [
            (prob[b] * (dot(g, vs[b], NT) - delta) * SCALE).astype(jnp.bfloat16) for b in range(3)
        ]
        far_send[0, h] = dot(score_grad[0], q, TN).astype(jnp.bfloat16)
        far_send[1, h] = dot(prob_half[0], g, TN).astype(jnp.bfloat16)
        outs[1, h] = sum(dot(score_grad[b], ks[b], NN) for b in range(3)).astype(jnp.bfloat16)
        near_terms[0, h] = dot(score_grad[1], q, TN)
        near_terms[1, h] = dot(prob_half[1], g, TN)
        own_terms[0, h] = dot(score_grad[2], q, TN)
        own_terms[1, h] = dot(prob_half[2], g, TN)
        for t in range(2):
            fterm_copy(t, h).start()
        for t in range(2):
            other_send[t, h] = own_terms[t, h, half(1 - core)].astype(jnp.bfloat16)

        @pl.when(h < heads - 2)
        def _():
            relay(h + 2)

        @pl.when(h > 0)
        def _():
            send_nterm(h - 1)

        for t in range(2):
            outs_copy(t, h).start()
            other_copy(t, h).start()
            store(t, h).start()
        return carry

    lax.fori_loop(0, heads, one_head, 0)
    send_nterm(heads - 1)

    for h in range(heads):
        for t in range(2):
            outs_copy(t, h).wait_recv()
            store_other(t, h).start()
            other_copy(t, h).wait_recv()

    for h in range(heads):
        for t in range(2):
            for c in range(2):
                j = c * heads + h
                remote(
                    near_send.at[t, h, half(c)],
                    near_got.at[t, j],
                    nterm_ssem.at[t, h, c],
                    nterm_rsem.at[t, j],
                    left,
                    core,
                ).wait_recv()
                mine = own_terms[t, h, half(core)]
                other = other_got[t, h].astype(jnp.float32)
                term = jnp.where(core == c, mine, other)
                result[t, j] = (term + near_got[t, j].astype(jnp.float32)).astype(jnp.bfloat16)
        for t in range(2):
            for c in range(2):
                result_copy(t, c * heads + h).start()

    for peer in peers:
        meta_copy(peer).wait_send()
    for h in range(heads):
        for t in range(4):
            own_copy(t, h).wait_send()
        for t in range(2):
            far_copy(h, t).wait_send()
            outs_copy(t, h).wait_send()
            other_copy(t, h).wait_send()
            fterm_copy(t, h).wait_send()
            store(t, h).wait()
            store_other(t, h).wait()
            for c in range(2):
                near_copy(h, c, t).wait_send()
                nterm_copy(t, h, c).wait_send()
                result_copy(t, c * heads + h).wait()


def solution(mesh):
    n_chip = mesh.shape["seq"] // 2

    def body(queries, keys, values, grad_out, doc_ids, loss_mask):
        rows, width = queries.shape
        heads = width // HEAD_DIM // 2
        D = HEAD_DIM
        bf16, f32 = jnp.bfloat16, jnp.float32
        dma = pltpu.SemaphoreType.DMA
        shape = jax.ShapeDtypeStruct((rows, width), bf16)
        vmem = pltpu.VMEM
        return pl.pallas_call(
            functools.partial(kernel, n_chip, rows, heads),
            out_shape=(shape,) * 4,
            in_specs=[pl.BlockSpec(memory_space=pl.ANY)] * 4 + [pl.BlockSpec(memory_space=pltpu.VMEM)] * 2,
            out_specs=(pl.BlockSpec(memory_space=pl.ANY),) * 4,
            scratch_shapes=[
                vmem((4, heads, 2 * rows, D), bf16),
                vmem((2, heads, 2 * rows, D), bf16),
                vmem((2, heads, 2 * rows, D), bf16),
                vmem((1, 128), jnp.int32),
                vmem((20, 1, 128), jnp.int32),
                vmem((2 * rows, 6 * rows), f32),
                vmem((2 * rows, 128), f32),
                vmem((2, heads, 2 * rows, D), bf16),
                vmem((2, heads, rows, D), bf16),
                vmem((2, heads, 2 * rows, D), f32),
                vmem((2, heads, 2 * rows, D), f32),
                vmem((2, heads, rows, D), bf16),
                vmem((2, heads, rows, D), bf16),
                vmem((2, heads, 2 * rows, D), bf16),
                vmem((2, heads, 2 * rows, D), bf16),
                vmem((2, heads, 2 * rows, D), bf16),
                vmem((2, 2 * heads, rows, D), bf16),
                vmem((2, 2 * heads, rows, D), bf16),
                dma((4, heads)),
                dma((4, heads)),
                dma((4, heads)),
                dma((heads, 2, 2)),
                dma((heads, 2, 2)),
                dma((heads, 2)),
                dma((heads, 2)),
                dma((20,)),
                dma((20,)),
                dma((2, heads)),
                dma((2, heads)),
                dma((4, 2 * heads)),
                dma((2, heads)),
                dma((2, heads)),
                dma((2, heads)),
                dma((2, heads)),
                dma((2, heads, 2)),
                dma((2, 2 * heads)),
            ],
            compiler_params=pltpu.CompilerParams(
                collective_id=0, has_side_effects=True, vmem_limit_bytes=60 * 1024 * 1024
            ),
        )(queries, keys, values, grad_out, doc_ids.reshape(1, -1), loss_mask.reshape(1, -1))

    return jax.shard_map(
        body,
        mesh=mesh,
        in_specs=(P("seq", "head"),) * 4 + (P(("seq", "head")),) * 2,
        out_specs=(P("seq", "head"),) * 4,
        check_vma=False,
    )
```

time: 210 us -> 72.1 us (0.34)
  the two profiles are of different devices: /device:TPU:255 before, /device:TPU:207 now
where the time goes in v1:
time: 72.1 us; the launch traced here: 71.9 us
  Pallas kernels  66.8 us (93%)
  local copies, waits for them, and re-layouts  4.5 us (6%)
    pallas_call x1, Pallas kernels, body(): pl.pallas_call(functools.partial(kernel, n_chip, rows, heads), out_shape=...  66.8 us
    unnamed x10, local copies, waits for them, and re-layouts  4.5 us

profile of v1, /device:TPU:207, one launch (start us, length us, event | category | flops | bytes accessed | tf_op | source)
XLA Modules:
  0.0 71.9 jit_solution(4165228417616807548)
XLA Ops:
  0.6 66.8 %shard_map.93 = (bf16[128,1024]{1,0:T(8,128)(2,1)}, bf16[128,1024]{1,0:T(8,128)(2,1)}, bf16[128,1024]{1,0:T(8,128)(2,1)}, bf16[128,1024]{1,0:T(8,128)(2,1)}) custom-call(bf16[128,1024]{1,0:T(8,128)(2,1)} %q_in.1, bf16[128,1024]{1,0:T(8,128)(2,1)} %k_in.1, bf16[128,1024]{1,0:T(8,128)(2,1)} %v_in.1, bf16[128,1024]{1,0:T(8,128)(2,1)} %g_in.1, s32[1,64]{1,0:T(1,128)} %bitcast.2, ...), custom_call_target="tpu_custom_call" | custom-call | tf_op jit(solution)/shard_map/pallas_call | solution.py:407
  67.4 0.0 copy-start.2
  67.4 1.7 %copy.14 = bf16[128,1024]{1,0:T(8,128)(2,1)} copy(bf16[128,1024]{1,0:T(8,128)(2,1)} %get-tuple-element.8) | data formatting | bytes 524288
  69.1 0.0 copy-done.2
  69.1 0.0 copy-start.1
  69.1 0.7 copy.15
  69.8 0.3 copy-done.1
  70.2 0.0 copy-start
  70.2 0.7 copy.16
  70.9 0.3 copy-done
  71.2 0.7 copy.17
Async XLA Ops:
  67.4 1.7 %copy-start.2 = (bf16[128,1024]{1,0:T(8,128)(2,1)S(1)}, bf16[128,1024]{1,0:T(8,128)(2,1)}, u32[]{:S(2)}) copy-start(bf16[128,1024]{1,0:T(8,128)(2,1)} %get-tuple-element.9) | copy-start | bytes 786436
  69.1 1.0 %copy-start.1 = (bf16[128,1024]{1,0:T(8,128)(2,1)S(1)}, bf16[128,1024]{1,0:T(8,128)(2,1)}, u32[]{:S(2)}) copy-start(bf16[128,1024]{1,0:T(8,128)(2,1)} %get-tuple-element.10) | copy-start | bytes 786436
  70.2 1.0 %copy-start = (bf16[128,1024]{1,0:T(8,128)(2,1)S(1)}, bf16[128,1024]{1,0:T(8,128)(2,1)}, u32[]{:S(2)}) copy-start(bf16[128,1024]{1,0:T(8,128)(2,1)} %get-tuple-element.11) | copy-start | bytes 786436

commit v2 on v1

--- a/solution.py
+++ b/solution.py
@@ -35,6 +35,8 @@
     qg_out,
     kg_out,
     vg_out,
+    kv_mine,
+    ids_mask,
     own,
     near,
     far,
@@ -52,8 +54,9 @@
     far_got,
     near_send,
     near_got,
-    result,
     load_sem,
+    kv_sem,
+    ids_sem,
     own_ssem,
     own_rsem,
     near_ssem,
@@ -64,7 +67,6 @@
     meta_rsem,
     outs_ssem,
     outs_rsem,
-    store_sem,
     other_ssem,
     other_rsem,
     fterm_ssem,
@@ -79,8 +81,18 @@
     right, left = lax.rem(chip + 1, n_chip), lax.rem(chip + n_chip - 1, n_chip)
     ins = (q_in, k_in, v_in, g_in)
 
+    has_left, has_left2 = chip >= 1, chip >= 2
+    has_right, has_right2 = chip <= n_chip - 2, chip <= n_chip - 3
+    exists = {-2: has_left2, -1: has_left, 1: has_right, 2: has_right2}
+
     def at_chip(offset):
         return lax.rem(chip + n_chip + offset, n_chip)
+
+    def where_chip(offset, act):
+        if offset == 0:
+            act()
+        else:
+            pl.when(exists[offset])(act)
 
     def half(which):
         return pl.ds(pl.multiple_of(which * rows, rows), rows)
@@ -97,15 +109,6 @@
             device_id=(to_chip * 2 + to_core, hd if to_hd is None else to_hd),
             device_id_type=MESH,
         )
-
-    def load(t, h):
-        return pltpu.make_async_copy(
-            ins[t].at[:, columns(core, h)], own.at[t, h, half(core)], load_sem.at[t, h]
-        )
-
-    for t in range(4):
-        for h in range(heads):
-            load(t, h).start()
 
     peers = []
     for offset in (-2, -1, 0, 1, 2):
@@ -118,24 +121,79 @@
                 else:
                     peers.append((offset, c, d))
 
+    def peers_at(offset):
+        return [peer for peer in peers if peer[0] == offset]
+
     barrier = pltpu.get_barrier_semaphore()
-    for offset, c, d in peers:
-        pl.semaphore_signal(
-            barrier, inc=1, device_id=(at_chip(offset) * 2 + c, d), device_id_type=MESH
-        )
-
-    packed = ids_in[...] * 2 + mask_in[...]
+    for offset in (-2, -1, 0, 1, 2):
+
+        @functools.partial(where_chip, offset)
+        def _(offset=offset):
+            for _, c, d in peers_at(offset):
+                pl.semaphore_signal(
+                    barrier, inc=1, device_id=(at_chip(offset) * 2 + c, d), device_id_type=MESH
+                )
+
+    def kv_load(t):
+        return pltpu.make_async_copy(ins[1 + t], kv_mine.at[t], kv_sem.at[t])
+
+    def ids_load(t):
+        return pltpu.make_async_copy((ids_in, mask_in)[t], ids_mask.at[t], ids_sem.at[t])
+
+    for t in range(2):
+        ids_load(t).start()
+        kv_load(t).start()
+
+    def load(t, h):
+        return pltpu.make_async_copy(
+            ins[t].at[:, columns(core, h)], own.at[t, h, half(core)], load_sem.at[t, h]
+        )
+
+    for t in range(4):
+        for h in range(heads):
+            load(t, h).start()
+
+    @pl.when(jnp.logical_not(has_left))
+    def _():
+        near[...] = jnp.zeros_like(near)
+
+    @pl.when(jnp.logical_not(has_left2))
+    def _():
+        far[...] = jnp.zeros_like(far)
+
+    @pl.when(jnp.logical_not(has_right))
+    def _():
+        near_got[...] = jnp.zeros_like(near_got)
+
+    @pl.when(jnp.logical_not(jnp.logical_and(has_left, has_right)))
+    def _():
+        far_got[...] = jnp.zeros_like(far_got)
+
+    for offset in (-2, -1, 1, 2):
+
+        @pl.when(jnp.logical_not(exists[offset]))
+        def _(offset=offset):
+            for c in range(2):
+                meta[(2 + offset) * 4 + c * 2] = jnp.full((1, 128), -2, jnp.int32)
+                meta[(2 + offset) * 4 + c * 2 + 1] = jnp.zeros((1, 128), jnp.int32)
+
+    for t in range(2):
+        ids_load(t).wait()
+    packed = ids_mask[0] * 2 + ids_mask[1]
     wide = jnp.concatenate([packed, packed], axis=1)
     lane = lax.broadcasted_iota(jnp.int32, (1, 128), 1)
     wide = jnp.where((lane // 64) == hd, wide, 0)
     meta_mine[...] = wide
     meta[8 + core * 2 + hd] = wide
 
-    pl.semaphore_wait(barrier, len(peers))
+    for t in range(2):
+        kv_load(t).wait()
+    there = sum(exists[offset].astype(jnp.int32) for offset in (-2, -1, 1, 2))
+    pl.semaphore_wait(barrier, 3 + 4 * there)
 
     def near_copy(h, c, t):
         return remote(
-            ins[1 + t].at[:, columns(c, h)],
+            kv_mine.at[t, :, columns(c, h)],
             near.at[t, h, half(core)],
             near_ssem.at[h, c, t],
             near_rsem.at[h, core, t],
@@ -148,20 +206,33 @@
             near.at[t, h, half(c)], near.at[t, h, half(c)], near_ssem.at[h, c, t], near_rsem.at[h, c, t], right, core
         )
 
-    def far_copy(h, t):
-        return remote(near.at[t, h], far.at[t, h], far_ssem.at[h, t], far_rsem.at[h, t], right, core)
+    def far_copy(h, c, t):
+        return remote(
+            near.at[t, h, half(c)],
+            far.at[t, h, half(c)],
+            far_ssem.at[h, c, t],
+            far_rsem.at[h, c, t],
+            right,
+            core,
+        )
 
     def send_near(h):
-        for t in range(2):
-            for c in range(2):
-                near_copy(h, c, t).start()
+        @pl.when(has_right)
+        def _():
+            for t in range(2):
+                for c in range(2):
+                    near_copy(h, c, t).start()
 
     def relay(h):
-        for c in range(2):
-            for t in range(2):
-                near_arrival(h, c, t).wait_recv()
-        for t in range(2):
-            far_copy(h, t).start()
+        @pl.when(has_left)
+        def _():
+            for t in range(2):
+                for c in range(2):
+                    near_arrival(h, c, t).wait_recv()
+
+                    @pl.when(has_right)
+                    def _():
+                        far_copy(h, c, t).start()
 
     def own_copy(t, h):
         return remote(
@@ -190,19 +261,26 @@
         place = (2 + offset) * 4 + c * 2 + d
         return remote(meta_mine, meta.at[place], meta_ssem.at[place], meta_rsem.at[place], at_chip(offset), c, d)
 
-    send_near(0)
-    for peer in peers:
-        meta_copy(peer).start()
+    for offset in (0, -1, 1, -2, 2):
+
+        @functools.partial(where_chip, offset)
+        def _(offset=offset):
+            for peer in peers_at(offset):
+                meta_copy(peer).start()
+
     for h in range(heads):
+        send_near(h)
         for t in range(4):
             own_copy(t, h).start()
-    send_near(1)
-
-    relay(0)
-    send_near(2)
-
-    for peer in peers:
-        meta_arrival(peer).wait_recv()
+    for h in range(heads):
+        relay(h)
+
+    for offset in (0, -1, 1, -2, 2):
+
+        @functools.partial(where_chip, offset)
+        def _(offset=offset):
+            for peer in peers_at(offset):
+                meta_arrival(peer).wait_recv()
 
     def row_of(place):
         return meta[4 * (place // 2) + 2 * (place % 2)] + meta[4 * (place // 2) + 2 * (place % 2) + 1]
@@ -243,9 +321,6 @@
                 1 - core,
             ).wait_recv()
 
-    relay(1)
-    send_near(3)
-
     def outs_copy(t, h):
         return remote(
             outs.at[t, h, half(1 - core)],
@@ -274,35 +349,41 @@
             c,
         )
 
-    def store(t, h):
-        return pltpu.make_async_copy(
-            outs.at[t, h, half(core)], (o_out, qg_out)[t].at[:, columns(core, h)], store_sem.at[t, core * heads + h]
-        )
-
-    def store_other(t, h):
-        return pltpu.make_async_copy(
-            outs_other.at[t, h],
-            (o_out, qg_out)[t].at[:, columns(1 - core, h)],
-            store_sem.at[t, (1 - core) * heads + h],
-        )
-
-    def result_copy(t, j):
-        return pltpu.make_async_copy(
-            result.at[t, j], (kg_out, vg_out)[t].at[:, pl.ds(j * D, D)], store_sem.at[2 + t, j]
-        )
-
     def send_nterm(h):
-        for t in range(2):
-            fterm_copy(t, h).wait_recv()
-        for t in range(2):
-            near_send[t, h] = (near_terms[t, h] + far_got[t, h].astype(jnp.float32)).astype(jnp.bfloat16)
-        for t in range(2):
-            for c in range(2):
-                nterm_copy(t, h, c).start()
+        @pl.when(jnp.logical_and(has_left, has_right))
+        def _():
+            for t in range(2):
+                fterm_copy(t, h).wait_recv()
+
+        @pl.when(has_left)
+        def _():
+            for t in range(2):
+                near_send[t, h] = (near_terms[t, h] + far_got[t, h].astype(jnp.float32)).astype(jnp.bfloat16)
+            for t in range(2):
+                for c in range(2):
+                    nterm_copy(t, h, c).start()
 
     def one_head(h, carry):
-        for t in range(2):
-            far_copy(h, t).wait_recv()
+        @pl.when(has_left2)
+        def _():
+            for t in range(2):
+                for c in range(2):
+                    far_copy(h, c, t).wait_recv()
+
+
+        @pl.when(jnp.logical_and(h == 3, jnp.logical_and(has_left2, lax.rem(chip, 4) == 0)))
+        def _():
+            for i in (0, 1, 2):
+                for t in range(2):
+                    fterm_copy(t, i).start()
+
+
+        @pl.when(jnp.logical_and(h == 3, jnp.logical_and(has_left2, lax.rem(chip, 4) != 0)))
+        def _():
+            for i in (0, 1):
+                for t in range(2):
+                    fterm_copy(t, i).start()
+
         q, g = own[0, h], (weight[...] * own[3, h].astype(jnp.float32)).astype(jnp.bfloat16)
         ks = (far[0, h], near[0, h], own[1, h])
         vs = (far[1, h], near[1, h], own[2, h])
@@ -328,69 +409,109 @@
         own_terms[0, h] = dot(score_grad[2], q, TN)
         own_terms[1, h] = dot(prob_half[2], g, TN)
         for t in range(2):
-            fterm_copy(t, h).start()
-        for t in range(2):
             other_send[t, h] = own_terms[t, h, half(1 - core)].astype(jnp.bfloat16)
-
-        @pl.when(h < heads - 2)
-        def _():
-            relay(h + 2)
-
-        @pl.when(h > 0)
-        def _():
-            send_nterm(h - 1)
 
         for t in range(2):
             outs_copy(t, h).start()
             other_copy(t, h).start()
-            store(t, h).start()
+            (o_out, qg_out)[t][:, columns(core, h)] = outs[t, h, half(core)]
         return carry
 
     lax.fori_loop(0, heads, one_head, 0)
-    send_nterm(heads - 1)
+    @pl.when(jnp.logical_and(has_left2, lax.rem(chip, 4) == 0))
+    def _():
+        for i in (3,):
+            for t in range(2):
+                fterm_copy(t, i).start()
+
+    @pl.when(jnp.logical_and(has_left2, lax.rem(chip, 4) != 0))
+    def _():
+        for i in (2, 3):
+            for t in range(2):
+                fterm_copy(t, i).start()
+
+    for h in range(heads):
+        send_nterm(h)
 
     for h in range(heads):
         for t in range(2):
             outs_copy(t, h).wait_recv()
-            store_other(t, h).start()
+            (o_out, qg_out)[t][:, columns(1 - core, h)] = outs_other[t, h]
             other_copy(t, h).wait_recv()
 
     for h in range(heads):
         for t in range(2):
             for c in range(2):
                 j = c * heads + h
-                remote(
-                    near_send.at[t, h, half(c)],
-                    near_got.at[t, j],
-                    nterm_ssem.at[t, h, c],
-                    nterm_rsem.at[t, j],
-                    left,
-                    core,
-                ).wait_recv()
+
+                @pl.when(has_right)
+                def _():
+                    remote(
+                        near_send.at[t, h, half(c)],
+                        near_got.at[t, j],
+                        nterm_ssem.at[t, h, c],
+                        nterm_rsem.at[t, j],
+                        left,
+                        core,
+                    ).wait_recv()
+
                 mine = own_terms[t, h, half(core)]
                 other = other_got[t, h].astype(jnp.float32)
                 term = jnp.where(core == c, mine, other)
-                result[t, j] = (term + near_got[t, j].astype(jnp.float32)).astype(jnp.bfloat16)
-        for t in range(2):
-            for c in range(2):
-                result_copy(t, c * heads + h).start()
-
-    for peer in peers:
-        meta_copy(peer).wait_send()
+                (kg_out, vg_out)[t][:, j * D : (j + 1) * D] = (
+                    term + near_got[t, j].astype(jnp.float32)
+                ).astype(jnp.bfloat16)
+
+    for offset in (-2, -1, 0, 1, 2):
+
+        @functools.partial(where_chip, offset)
+        def _(offset=offset):
+            for peer in peers_at(offset):
+                meta_copy(peer).wait_send()
+
     for h in range(heads):
         for t in range(4):
             own_copy(t, h).wait_send()
         for t in range(2):
-            far_copy(h, t).wait_send()
             outs_copy(t, h).wait_send()
             other_copy(t, h).wait_send()
-            fterm_copy(t, h).wait_send()
-            store(t, h).wait()
-            store_other(t, h).wait()
-            for c in range(2):
-                near_copy(h, c, t).wait_send()
-                nterm_copy(t, h, c).wait_send()
-                result_copy(t, c * heads + h).wait()
+
+    @pl.when(has_right)
+    def _():
+        for h in range(heads):
+            for t in range(2):
+                for c in range(2):
+                    near_copy(h, c, t).wait_send()
+
+    @pl.when(jnp.logical_and(has_left, has_right))
+    def _():
+        for h in range(heads):
+            for t in range(2):
+                for c in range(2):
+                    far_copy(h, c, t).wait_send()
+
+    @pl.when(has_left2)
+    def _():
+        for h in range(heads):
+            for t in range(2):
+                fterm_copy(t, h).wait_send()
+
+    @pl.when(has_left)
+    def _():
+        for h in range(heads):
+            for t in range(2):
+                for c in range(2):
+                    nterm_copy(t, h, c).wait_send()
+
+
+def write_kernel(*refs):
+    sems = refs[-1]
+    n = (len(refs) - 1) // 2
+    copies = [pltpu.make_async_copy(refs[i], refs[n + i], sems.at[i]) for i in range(n)]
+    for copy in copies:
+        copy.start()
+    for copy in copies:
+        copy.wait()
 
 
 def solution(mesh):
@@ -404,12 +525,14 @@
         dma = pltpu.SemaphoreType.DMA
         shape = jax.ShapeDtypeStruct((rows, width), bf16)
         vmem = pltpu.VMEM
-        return pl.pallas_call(
+        held = pl.pallas_call(
             functools.partial(kernel, n_chip, rows, heads),
-            out_shape=(shape,) * 4,
-            in_specs=[pl.BlockSpec(memory_space=pl.ANY)] * 4 + [pl.BlockSpec(memory_space=pltpu.VMEM)] * 2,
-            out_specs=(pl.BlockSpec(memory_space=pl.ANY),) * 4,
+            out_shape=(pltpu.VMEM((rows, width), bf16),) * 4,
+            in_specs=[pl.BlockSpec(memory_space=pl.ANY)] * 6,
+            out_specs=(pl.BlockSpec(memory_space=pltpu.VMEM),) * 4,
             scratch_shapes=[
+                vmem((2, rows, width), bf16),
+                vmem((2, 1, 64), jnp.int32),
                 vmem((4, heads, 2 * rows, D), bf16),
                 vmem((2, heads, 2 * rows, D), bf16),
                 vmem((2, heads, 2 * rows, D), bf16),
@@ -427,19 +550,19 @@
                 vmem((2, heads, 2 * rows, D), bf16),
                 vmem((2, heads, 2 * rows, D), bf16),
                 vmem((2, 2 * heads, rows, D), bf16),
-                vmem((2, 2 * heads, rows, D), bf16),
                 dma((4, heads)),
+                dma((2,)),
+                dma((2,)),
                 dma((4, heads)),
                 dma((4, heads)),
                 dma((heads, 2, 2)),
                 dma((heads, 2, 2)),
-                dma((heads, 2)),
-                dma((heads, 2)),
+                dma((heads, 2, 2)),
+                dma((heads, 2, 2)),
                 dma((20,)),
                 dma((20,)),
                 dma((2, heads)),
                 dma((2, heads)),
-                dma((4, 2 * heads)),
                 dma((2, heads)),
                 dma((2, heads)),
                 dma((2, heads)),
@@ -451,6 +574,13 @@
                 collective_id=0, has_side_effects=True, vmem_limit_bytes=60 * 1024 * 1024
             ),
         )(queries, keys, values, grad_out, doc_ids.reshape(1, -1), loss_mask.reshape(1, -1))
+        return pl.pallas_call(
+            write_kernel,
+            out_shape=(shape,) * 4,
+            in_specs=[pl.BlockSpec(memory_space=pltpu.VMEM)] * 4,
+            out_specs=(pl.BlockSpec(memory_space=pl.ANY),) * 4,
+            scratch_shapes=[dma((4,))],
+        )(*(pltpu.with_memory_space_constraint(x, pltpu.VMEM) for x in held))
 
     return jax.shard_map(
         body,

time: 72.1 us -> 65.2 us (0.904)
  the two profiles are of different devices: /device:TPU:207 before, /device:TPU:255 now
where the time goes in v2:
time: 65.2 us; the launch traced here: 65.1 us
  Pallas kernels  64.4 us (99%)
    pallas_call x1, Pallas kernels, body(): pl.pallas_call(functools.partial(kernel, n_chip, rows, heads), out_shape=...  63.4 us

profile of v2, /device:TPU:255, one launch (start us, length us, event | category | flops | bytes accessed | tf_op | source)
XLA Modules:
  0.0 65.1 jit_solution(3958453328351275663)
XLA Ops:
  0.6 63.4 %shard_map.93 = (bf16[128,1024]{1,0:T(8,128)(2,1)S(1)}, bf16[128,1024]{1,0:T(8,128)(2,1)S(1)}, bf16[128,1024]{1,0:T(8,128)(2,1)S(1)}, bf16[128,1024]{1,0:T(8,128)(2,1)S(1)}) custom-call(bf16[128,1024]{1,0:T(8,128)(2,1)} %q_in.1, bf16[128,1024]{1,0:T(8,128)(2,1)} %k_in.1, bf16[128,1024]{1,0:T(8,128)(2,1)} %v_in.1, bf16[128,1024]{1,0:T(8,128)(2,1)} %g_in.1, ...), custom_call_target="tpu_custom_call" | custom-call | tf_op jit(solution)/shard_map/pallas_call | solution.py:528
  64.1 1.0 %shard_map.94 = (bf16[128,1024]{1,0:T(8,128)(2,1)}, bf16[128,1024]{1,0:T(8,128)(2,1)}, bf16[128,1024]{1,0:T(8,128)(2,1)}, bf16[128,1024]{1,0:T(8,128)(2,1)}) custom-call(bf16[128,1024]{1,0:T(8,128)(2,1)S(1)} %get-tuple-element.8.refs_0_, bf16[128,1024]{1,0:T(8,128)(2,1)S(1)} %get-tuple-element.9.refs_1_, bf16[128,1024]{1,0:T(8,128)(2,1)S(1)} %get-tuple-element.10.refs_2_, ...), custom_call_target="tpu_custom_call" | custom-call | tf_op jit(solution)/shard_map/pallas_call | solution.py:577

commit v3 on v2

--- a/solution.py
+++ b/solution.py
@@ -40,7 +40,6 @@
     own,
     near,
     far,
-    meta_mine,
     meta,
     bias,
     weight,
@@ -63,8 +62,12 @@
     near_rsem,
     far_ssem,
     far_rsem,
-    meta_ssem,
-    meta_rsem,
+    half_ssem,
+    half_rsem,
+    rows_ssem,
+    rows_rsem,
+    past_ssem,
+    past_rsem,
     outs_ssem,
     outs_rsem,
     other_ssem,
@@ -110,29 +113,20 @@
             device_id_type=MESH,
         )
 
-    peers = []
-    for offset in (-2, -1, 0, 1, 2):
-        for c in range(2):
-            for d in range(2):
-                if offset == 0:
-                    if c == 0 and d == 0:
-                        continue
-                    peers.append((0, lax.rem(core + c, 2), lax.rem(hd + d, 2)))
-                else:
-                    peers.append((offset, c, d))
-
-    def peers_at(offset):
-        return [peer for peer in peers if peer[0] == offset]
-
     barrier = pltpu.get_barrier_semaphore()
-    for offset in (-2, -1, 0, 1, 2):
+
+    def greet(to_chip, to_core, to_hd):
+        pl.semaphore_signal(barrier, inc=1, device_id=(to_chip * 2 + to_core, to_hd), device_id_type=MESH)
+
+    for offset in (-1, 1):
 
         @functools.partial(where_chip, offset)
         def _(offset=offset):
-            for _, c, d in peers_at(offset):
-                pl.semaphore_signal(
-                    barrier, inc=1, device_id=(at_chip(offset) * 2 + c, d), device_id_type=MESH
-                )
+            for c in range(2):
+                greet(at_chip(offset), c, hd)
+
+    greet(chip, 1 - core, hd)
+    greet(chip, core, 1 - hd)
 
     def kv_load(t):
         return pltpu.make_async_copy(ins[1 + t], kv_mine.at[t], kv_sem.at[t])
@@ -183,13 +177,12 @@
     wide = jnp.concatenate([packed, packed], axis=1)
     lane = lax.broadcasted_iota(jnp.int32, (1, 128), 1)
     wide = jnp.where((lane // 64) == hd, wide, 0)
-    meta_mine[...] = wide
     meta[8 + core * 2 + hd] = wide
 
     for t in range(2):
         kv_load(t).wait()
-    there = sum(exists[offset].astype(jnp.int32) for offset in (-2, -1, 1, 2))
-    pl.semaphore_wait(barrier, 3 + 4 * there)
+    there = exists[-1].astype(jnp.int32) + exists[1].astype(jnp.int32)
+    pl.semaphore_wait(barrier, 2 + 2 * there)
 
     def near_copy(h, c, t):
         return remote(
@@ -244,43 +237,76 @@
             1 - core,
         )
 
-    def meta_copy(peer):
-        offset, c, d = peer
-        return remote(
-            meta_mine,
-            meta.at[(2 - offset) * 4 + core * 2 + hd],
-            meta_ssem.at[(2 + offset) * 4 + c * 2 + d],
-            meta_rsem.at[(2 - offset) * 4 + core * 2 + hd],
+    def half_copy():
+        mine = meta.at[8 + core * 2 + hd]
+        return remote(mine, mine, half_ssem.at[0], half_rsem.at[0], chip, core, 1 - hd)
+
+    def rows_copy(offset, c):
+        return remote(
+            meta.at[pl.ds(8 + core * 2, 2)],
+            meta.at[pl.ds((2 - offset) * 4 + core * 2, 2)],
+            rows_ssem.at[1 + offset, c],
+            rows_rsem.at[1 - offset, core],
             at_chip(offset),
             c,
-            d,
-        )
-
-    def meta_arrival(peer):
-        offset, c, d = peer
-        place = (2 + offset) * 4 + c * 2 + d
-        return remote(meta_mine, meta.at[place], meta_ssem.at[place], meta_rsem.at[place], at_chip(offset), c, d)
-
-    for offset in (0, -1, 1, -2, 2):
-
-        @functools.partial(where_chip, offset)
-        def _(offset=offset):
-            for peer in peers_at(offset):
-                meta_copy(peer).start()
-
+        )
+
+    def rows_arrival(offset, c):
+        rows_there = meta.at[pl.ds((2 + offset) * 4 + c * 2, 2)]
+        return remote(rows_there, rows_there, rows_ssem.at[1 + offset, c], rows_rsem.at[1 + offset, c], chip, 1 - core)
+
+    def past_copy(offset):
+        return remote(
+            meta.at[pl.ds((2 - offset) * 4, 4)],
+            meta.at[pl.ds((2 - 2 * offset) * 4, 4)],
+            past_ssem.at[(1 - offset) // 2],
+            past_rsem.at[(1 - offset) // 2],
+            at_chip(offset),
+            core,
+        )
+
+    def rows_to(offset, act):
+        if offset == 0:
+            act(0, 1 - core)
+        else:
+
+            @pl.when(exists[offset])
+            def _():
+                for c in range(2):
+                    act(offset, c)
+
+    inner = jnp.logical_and(has_left, has_right)
+
+    half_copy().start()
+    send_near(0)
+    send_near(1)
+    half_copy().wait_recv()
+    for offset in (0, 1, -1):
+        rows_to(offset, lambda offset, c: rows_copy(offset, c).start())
     for h in range(heads):
-        send_near(h)
         for t in range(4):
             own_copy(t, h).start()
-    for h in range(heads):
+    send_near(2)
+    relay(0)
+    for offset in (0, 1, -1):
+        rows_to(offset, lambda offset, c: rows_arrival(offset, c).wait_recv())
+
+    @pl.when(inner)
+    def _():
+        past_copy(1).start()
+        past_copy(-1).start()
+
+    send_near(3)
+    for h in range(1, heads):
         relay(h)
 
-    for offset in (0, -1, 1, -2, 2):
-
-        @functools.partial(where_chip, offset)
-        def _(offset=offset):
-            for peer in peers_at(offset):
-                meta_arrival(peer).wait_recv()
+    @pl.when(has_left2)
+    def _():
+        past_copy(1).wait_recv()
+
+    @pl.when(has_right2)
+    def _():
+        past_copy(-1).wait_recv()
 
     def row_of(place):
         return meta[4 * (place // 2) + 2 * (place % 2)] + meta[4 * (place // 2) + 2 * (place % 2) + 1]
@@ -370,15 +396,7 @@
                 for c in range(2):
                     far_copy(h, c, t).wait_recv()
 
-
-        @pl.when(jnp.logical_and(h == 3, jnp.logical_and(has_left2, lax.rem(chip, 4) == 0)))
-        def _():
-            for i in (0, 1, 2):
-                for t in range(2):
-                    fterm_copy(t, i).start()
-
-
-        @pl.when(jnp.logical_and(h == 3, jnp.logical_and(has_left2, lax.rem(chip, 4) != 0)))
+        @pl.when(jnp.logical_and(h == 2, jnp.logical_and(has_left2, lax.rem(chip, 4) == 0)))
         def _():
             for i in (0, 1):
                 for t in range(2):
@@ -408,6 +426,19 @@
         near_terms[1, h] = dot(prob_half[1], g, TN)
         own_terms[0, h] = dot(score_grad[2], q, TN)
         own_terms[1, h] = dot(prob_half[2], g, TN)
+
+        @pl.when(jnp.logical_and(h == 2, jnp.logical_and(has_left2, lax.rem(chip, 4) == 0)))
+        def _():
+            for i in (2,):
+                for t in range(2):
+                    fterm_copy(t, i).start()
+
+
+        @pl.when(jnp.logical_and(has_left2, lax.rem(chip, 4) != 0))
+        def _():
+            for t in range(2):
+                fterm_copy(t, h).start()
+
         for t in range(2):
             other_send[t, h] = own_terms[t, h, half(1 - core)].astype(jnp.bfloat16)
 
@@ -421,12 +452,6 @@
     @pl.when(jnp.logical_and(has_left2, lax.rem(chip, 4) == 0))
     def _():
         for i in (3,):
-            for t in range(2):
-                fterm_copy(t, i).start()
-
-    @pl.when(jnp.logical_and(has_left2, lax.rem(chip, 4) != 0))
-    def _():
-        for i in (2, 3):
             for t in range(2):
                 fterm_copy(t, i).start()
 
@@ -462,12 +487,14 @@
                     term + near_got[t, j].astype(jnp.float32)
                 ).astype(jnp.bfloat16)
 
-    for offset in (-2, -1, 0, 1, 2):
-
-        @functools.partial(where_chip, offset)
-        def _(offset=offset):
-            for peer in peers_at(offset):
-                meta_copy(peer).wait_send()
+    half_copy().wait_send()
+    for offset in (0, 1, -1):
+        rows_to(offset, lambda offset, c: rows_copy(offset, c).wait_send())
+
+    @pl.when(inner)
+    def _():
+        past_copy(1).wait_send()
+        past_copy(-1).wait_send()
 
     for h in range(heads):
         for t in range(4):
@@ -536,7 +563,6 @@
                 vmem((4, heads, 2 * rows, D), bf16),
                 vmem((2, heads, 2 * rows, D), bf16),
                 vmem((2, heads, 2 * rows, D), bf16),
-                vmem((1, 128), jnp.int32),
                 vmem((20, 1, 128), jnp.int32),
                 vmem((2 * rows, 6 * rows), f32),
                 vmem((2 * rows, 128), f32),
@@ -559,8 +585,12 @@
                 dma((heads, 2, 2)),
                 dma((heads, 2, 2)),
                 dma((heads, 2, 2)),
-                dma((20,)),
-                dma((20,)),
+                dma((1,)),
+                dma((1,)),
+                dma((3, 2)),
+                dma((3, 2)),
+                dma((2,)),
+                dma((2,)),
                 dma((2, heads)),
                 dma((2, heads)),
                 dma((2, heads)),

time: 65.2 us -> 62.2 us (0.954)
  Pallas kernels: 64.4 us -> 61.4 us
    pallas_call x1, Pallas kernels: 63.4 us -> 60.4 us  [body(): pl.pallas_call(functools.partial(kernel, n_chip, rows, heads), out_shape=...]
where the time goes in v3:
time: 62.2 us; the launch traced here: 62 us
  Pallas kernels  61.4 us (99%)
  between operations  0.64 us (1%)
    pallas_call x1, Pallas kernels, body(): pl.pallas_call(functools.partial(kernel, n_chip, rows, heads), out_shape=...  60.4 us

profile of v3, /device:TPU:255, one launch (start us, length us, event | category | flops | bytes accessed | tf_op | source)
XLA Modules:
  0.0 62.0 jit_solution(5278204050492904228)
XLA Ops:
  0.6 60.4 %shard_map.93 = (bf16[128,1024]{1,0:T(8,128)(2,1)S(1)}, bf16[128,1024]{1,0:T(8,128)(2,1)S(1)}, bf16[128,1024]{1,0:T(8,128)(2,1)S(1)}, bf16[128,1024]{1,0:T(8,128)(2,1)S(1)}) custom-call(bf16[128,1024]{1,0:T(8,128)(2,1)} %q_in.1, bf16[128,1024]{1,0:T(8,128)(2,1)} %k_in.1, bf16[128,1024]{1,0:T(8,128)(2,1)} %v_in.1, bf16[128,1024]{1,0:T(8,128)(2,1)} %g_in.1, ...), custom_call_target="tpu_custom_call" | custom-call | tf_op jit(solution)/shard_map/pallas_call | solution.py:555
  61.0 1.0 %shard_map.94 = (bf16[128,1024]{1,0:T(8,128)(2,1)}, bf16[128,1024]{1,0:T(8,128)(2,1)}, bf16[128,1024]{1,0:T(8,128)(2,1)}, bf16[128,1024]{1,0:T(8,128)(2,1)}) custom-call(bf16[128,1024]{1,0:T(8,128)(2,1)S(1)} %get-tuple-element.8.refs_0_, bf16[128,1024]{1,0:T(8,128)(2,1)S(1)} %get-tuple-element.9.refs_1_, bf16[128,1024]{1,0:T(8,128)(2,1)S(1)} %get-tuple-element.10.refs_2_, ...), custom_call_target="tpu_custom_call" | custom-call | tf_op jit(solution)/shard_map/pallas_call | solution.py:607

commit v4 on v3

--- a/solution.py
+++ b/solution.py
@@ -396,12 +396,6 @@
                 for c in range(2):
                     far_copy(h, c, t).wait_recv()
 
-        @pl.when(jnp.logical_and(h == 2, jnp.logical_and(has_left2, lax.rem(chip, 4) == 0)))
-        def _():
-            for i in (0, 1):
-                for t in range(2):
-                    fterm_copy(t, i).start()
-
         q, g = own[0, h], (weight[...] * own[3, h].astype(jnp.float32)).astype(jnp.bfloat16)
         ks = (far[0, h], near[0, h], own[1, h])
         vs = (far[1, h], near[1, h], own[2, h])
@@ -427,14 +421,7 @@
         own_terms[0, h] = dot(score_grad[2], q, TN)
         own_terms[1, h] = dot(prob_half[2], g, TN)
 
-        @pl.when(jnp.logical_and(h == 2, jnp.logical_and(has_left2, lax.rem(chip, 4) == 0)))
-        def _():
-            for i in (2,):
-                for t in range(2):
-                    fterm_copy(t, i).start()
-
-
-        @pl.when(jnp.logical_and(has_left2, lax.rem(chip, 4) != 0))
+        @pl.when(has_left2)
         def _():
             for t in range(2):
                 fterm_copy(t, h).start()
@@ -449,12 +436,6 @@
         return carry
 
     lax.fori_loop(0, heads, one_head, 0)
-    @pl.when(jnp.logical_and(has_left2, lax.rem(chip, 4) == 0))
-    def _():
-        for i in (3,):
-            for t in range(2):
-                fterm_copy(t, i).start()
-
     for h in range(heads):
         send_nterm(h)
 

time: 62.2 us -> 60.4 us (0.971)
  Pallas kernels: 61.4 us -> 59.6 us
    pallas_call x1, Pallas kernels: 60.4 us -> 58.6 us  [body(): pl.pallas_call(functools.partial(kernel, n_chip, rows, heads), out_shape=...]
where the time goes in v4:
time: 60.4 us; the launch traced here: 60.3 us
  Pallas kernels  59.6 us (99%)
  between operations  0.64 us (1%)
    pallas_call x1, Pallas kernels, body(): pl.pallas_call(functools.partial(kernel, n_chip, rows, heads), out_shape=...  58.6 us

profile of v4, /device:TPU:255, one launch (start us, length us, event | category | flops | bytes accessed | tf_op | source)
XLA Modules:
  0.0 60.3 jit_solution(7676262370783220988)
XLA Ops:
  0.6 58.6 %shard_map.93 = (bf16[128,1024]{1,0:T(8,128)(2,1)S(1)}, bf16[128,1024]{1,0:T(8,128)(2,1)S(1)}, bf16[128,1024]{1,0:T(8,128)(2,1)S(1)}, bf16[128,1024]{1,0:T(8,128)(2,1)S(1)}) custom-call(bf16[128,1024]{1,0:T(8,128)(2,1)} %q_in.1, bf16[128,1024]{1,0:T(8,128)(2,1)} %k_in.1, bf16[128,1024]{1,0:T(8,128)(2,1)} %v_in.1, bf16[128,1024]{1,0:T(8,128)(2,1)} %g_in.1, ...), custom_call_target="tpu_custom_call" | custom-call | tf_op jit(solution)/shard_map/pallas_call | solution.py:536
  59.3 1.0 %shard_map.94 = (bf16[128,1024]{1,0:T(8,128)(2,1)}, bf16[128,1024]{1,0:T(8,128)(2,1)}, bf16[128,1024]{1,0:T(8,128)(2,1)}, bf16[128,1024]{1,0:T(8,128)(2,1)}) custom-call(bf16[128,1024]{1,0:T(8,128)(2,1)S(1)} %get-tuple-element.8.refs_0_, bf16[128,1024]{1,0:T(8,128)(2,1)S(1)} %get-tuple-element.9.refs_1_, bf16[128,1024]{1,0:T(8,128)(2,1)S(1)} %get-tuple-element.10.refs_2_, ...), custom_call_target="tpu_custom_call" | custom-call | tf_op jit(solution)/shard_map/pallas_call | solution.py:588

commit v5 on v4

--- a/solution.py
+++ b/solution.py
@@ -287,6 +287,7 @@
         for t in range(4):
             own_copy(t, h).start()
     send_near(2)
+    send_near(3)
     relay(0)
     for offset in (0, 1, -1):
         rows_to(offset, lambda offset, c: rows_arrival(offset, c).wait_recv())
@@ -296,7 +297,6 @@
         past_copy(1).start()
         past_copy(-1).start()
 
-    send_near(3)
     for h in range(1, heads):
         relay(h)
 

time: 60.4 us -> 59.1 us (0.978)
  the two profiles are of different devices: /device:TPU:255 before, /device:TPU:223 now
where the time goes in v5:
time: 59.1 us; the launch traced here: 59 us
  Pallas kernels  58.4 us (99%)
  between operations  0.64 us (1%)
    pallas_call x1, Pallas kernels, body(): pl.pallas_call(functools.partial(kernel, n_chip, rows, heads), out_shape=...  57.4 us

profile of v5, /device:TPU:223, one launch (start us, length us, event | category | flops | bytes accessed | tf_op | source)
XLA Modules:
  0.0 59.0 jit_solution(13828308032288528740)
XLA Ops:
  0.6 57.4 %shard_map.93 = (bf16[128,1024]{1,0:T(8,128)(2,1)S(1)}, bf16[128,1024]{1,0:T(8,128)(2,1)S(1)}, bf16[128,1024]{1,0:T(8,128)(2,1)S(1)}, bf16[128,1024]{1,0:T(8,128)(2,1)S(1)}) custom-call(bf16[128,1024]{1,0:T(8,128)(2,1)} %q_in.1, bf16[128,1024]{1,0:T(8,128)(2,1)} %k_in.1, bf16[128,1024]{1,0:T(8,128)(2,1)} %v_in.1, bf16[128,1024]{1,0:T(8,128)(2,1)} %g_in.1, ...), custom_call_target="tpu_custom_call" | custom-call | tf_op jit(solution)/shard_map/pallas_call | solution.py:536
  58.0 1.0 %shard_map.94 = (bf16[128,1024]{1,0:T(8,128)(2,1)}, bf16[128,1024]{1,0:T(8,128)(2,1)}, bf16[128,1024]{1,0:T(8,128)(2,1)}, bf16[128,1024]{1,0:T(8,128)(2,1)}) custom-call(bf16[128,1024]{1,0:T(8,128)(2,1)S(1)} %get-tuple-element.8.refs_0_, bf16[128,1024]{1,0:T(8,128)(2,1)S(1)} %get-tuple-element.9.refs_1_, bf16[128,1024]{1,0:T(8,128)(2,1)S(1)} %get-tuple-element.10.refs_2_, ...), custom_call_target="tpu_custom_call" | custom-call | tf_op jit(solution)/shard_map/pallas_call | solution.py:588
